TPU v7x, 128 devices: a whole 4x4x4 slice. The times are simulated.
128 devices in a mesh: sims: 4 (over x_lo, core), ell: 32 (over x_hi, z, y).
Axes of the slice: x: 4 (x_hi: 2, x_lo: 2; x = x_hi * 2 + x_lo), y: 4, z: 4, core: 2. Of those that a mesh axis runs over, the one named last changes fastest.
Arguments:
- spectra: float32 [3, 6144, 896], P(None, 'ell', 'sims'), parts along dimension 2, may hold values from -6 to 6
- tables: float32 [3, 6144, 6144], P(None, 'ell'), may hold values from -0.15625 to 0.15625
- apodization: float32 [6144], replicated, may hold values from 0.2 to 1
- inv_mask: float32 [6144], replicated, may hold values from 0.5 to 4
- weights: float32 [6144], replicated, may hold values from 0.5 to 1.5
Outputs:
- corrected: float32 [3, 6144, 896], P(None, 'ell', 'sims'), parts along dimension 2
There are 4 independent parts, one for each index of `sims`. A program takes and returns all parts, laid end to end along the dimension named above; an argument that names none is the same for every part. Nothing has to cross between parts.
All inputs are finite; a program needn't handle non-finite values.
Results may differ from a plain program's by a relative error of at most 0.000094.
Values sent between devices are 32-bit elements; how exact they have to be, the bound alone decides.
A program may use at most 128 MiB of HBM per device.

v0:
```python
import jax
import jax.numpy as jnp
from jax import lax
from jax.sharding import PartitionSpec as P


def local(spectra, tables, apodization, inv_mask, weights):
    highest = lax.Precision.HIGHEST
    combined = jnp.stack([spectra[0], spectra[1] + spectra[2], spectra[1] - spectra[2]])
    factor = weights * apodization * inv_mask
    partial_corr = jnp.einsum("pla,pls->aps", tables, combined, precision=highest)
    total = lax.psum(partial_corr, "ell")
    fixed = total * factor[:, None, None]
    back = jnp.einsum("pla,aps->pls", tables, fixed, precision=highest)
    return jnp.stack([back[0], 0.5 * (back[1] + back[2]), 0.5 * (back[1] - back[2])])


def solution(mesh):
    placed = (P(None, "ell", "sims"), P(None, "ell", None), P(), P(), P())
    return jax.shard_map(
        local, mesh=mesh, in_specs=placed, out_specs=P(None, "ell", "sims"), check_vma=False
    )
```

profile of v0, /device:TPU:0, one launch (start us, length us, event | category | flops | bytes accessed | tf_op | source)
XLA Modules:
  0.0 490.3 jit_solution(4751571613912085866)
XLA Ops:
  6.5 0.0 all-reduce.2.cloned.1.call-start
  6.5 1.2 fusion.13
  7.7 0.0 copy-start
  7.7 0.0 copy-start.1
  7.7 0.0 copy-start.2
  7.7 19.2 %convolution_bitcast_fusion = f32[6144,3,224]{0,2,1:T(8,128)} fusion(f32[3,192,6144]{2,1,0:T(8,128)} %param.6, f32[1,192,224]{2,1,0:T(8,128)S(1)} %get-tuple-element.10, f32[1,192,224]{2,1,0:T(8,128)S(1)} %get-tuple-element.9, f32[1,192,224]{2,1,0:T(8,128)S(1)} %get-tuple-element.8), kind=kOutput, calls=%fused_computation.2 | convolution fusion | flops 9512939520 | bytes 31186944 | tf_op jit(solution)/shard_map/pla,pls->aps/dot_general | solution.py:11
  27.0 0.0 all-reduce.2.cloned.1.call-update
  27.0 0.0 copy-done
  27.0 0.0 copy-done.1
  27.0 0.0 copy-done.2
  27.0 432.5 %all-reduce.2.cloned.1.call-done = f32[6144,3,224]{0,2,1:T(8,128)} async-done(((f32[6144,3,224]{0,2,1:T(8,128)}), f32[6144,3,224]{0,2,1:T(8,128)}) %all-reduce.2.cloned.1.call-update) | async-done | bytes 16515088 | tf_op jit(solution)/shard_map/psum | solution.py:12
  459.6 23.0 %fusion.3 = f32[3,192,224]{2,1,0:T(8,128)S(1)} fusion(f32[3,192,6144]{2,1,0:T(8,128)} %param.6, f32[6144,3,224]{0,2,1:T(8,128)} %all-reduce.2.cloned.1.call-done, f32[6144]{0:T(1024)S(1)} %multiply_multiply_fusion), kind=kOutput, calls=%fused_computation.4 | convolution fusion | flops 9516810240 | bytes 31211520 | tf_op jit(solution)/shard_map/pla,aps->pls/dot_general | solution.py:14
  482.6 0.9 pad_maximum_fusion
  (2 shorter events, 0.1 us)
Async XLA Ops:
  6.5 453.0 %all-reduce.2.cloned.1.call-start = ((), (), s32[]{:S(2)}) async-start(), calls=%async_computation | async-start | bytes 33030144 | tf_op jit(solution)/shard_map/psum | solution.py:12
  7.7 19.3 %copy-start = (f32[6144]{0:T(1024)S(1)}, f32[6144]{0:T(1024)}, u32[]{:S(2)}) copy-start(f32[6144]{0:T(1024)} %param.8) | copy-start | bytes 73732
  7.7 19.3 %copy-start.1 = (f32[6144]{0:T(1024)S(1)}, f32[6144]{0:T(1024)}, u32[]{:S(2)}) copy-start(f32[6144]{0:T(1024)} %param.9) | copy-start | bytes 73732
  7.7 19.3 %copy-start.2 = (f32[6144]{0:T(1024)S(1)}, f32[6144]{0:T(1024)}, u32[]{:S(2)}) copy-start(f32[6144]{0:T(1024)} %param.7) | copy-start | bytes 73732
Sparse Core Ops, SparseCore 0:
  27.1 432.4 all-reduce.1
where the time goes:
time: 490 us
  waiting for transfers between devices  433 us (88%)
  matrix products  42.2 us (9%)
  between operations  13.5 us (3%)
    psum x1, waiting for transfers between devices, local(): total = lax.psum(partial_corr, 'ell')  433 us
    dot_general x1, matrix products, local(): back = jnp.einsum('pla,aps->pls', tables, fixed, precision=highest)  23 us
    dot_general x1, matrix products, local(): jnp.einsum('pla,pls->aps', tables, combined, precision=highest)  19.2 us
  transfers between devices with their start and end apart: 1, of which 1 were waited for; matrix products, arithmetic and copies ran while one was open for 0% of the time, Pallas kernels for 0%

commit v1 on v0

v1 whole, which is shorter than its diff:
```python
import jax
import jax.numpy as jnp
from jax import lax
from jax.experimental import pallas as pl
from jax.experimental.pallas import tpu as pltpu
from jax.sharding import PartitionSpec as P

WIDTH = 256
SLOTS = 4
DELAY = dict(relay=1, share=2, pass_on=3, corr=4, fold=5, total=6, scale=7,
             spread=8, back=9, ret=10, ret_fold=11, ret_sum=12)
F32, BF16 = jnp.float32, jnp.bfloat16


def split(x):
    high = x.astype(BF16)
    return high, (x - high.astype(F32)).astype(BF16)


def dot3(a, b, dims):
    def dot(u, v):
        return lax.dot_general(u, v, (dims, ((), ())), preferred_element_type=F32)

    return dot(a[0], b[0]) + (dot(a[0], b[1]) + dot(a[1], b[0]))


def kernel(spec, tables, weights, apod, inv_mask, out, tbl, relay, coef, corr, near,
           part, other, tot, fixed, back, ret1, ret2, own_sem, send, recv, p_send, p_recv):
    sims, ell = lax.axis_index("sims"), lax.axis_index("ell")
    y, z, x = lax.rem(ell, 4), lax.rem(lax.div(ell, 4), 4), lax.div(ell, 16)
    depth, nsim = out.shape[1], out.shape[2]
    span = tbl.shape[3]
    per = span // WIDTH
    chunks = 3 * per
    quarter, eighth = depth // 4, depth // 8
    group = nsim // 4
    half_w, half_d, half_s = WIDTH // 2, depth // 2, nsim // 2

    def ring(v, d):
        return lax.rem(v + d, 4)

    def at_y(d):
        return (sims, (x * 4 + z) * 4 + ring(y, d))

    def at_z(d):
        return (sims, (x * 4 + ring(z, d)) * 4 + y)

    y_up, y_down, z_up, z_down = at_y(1), at_y(3), at_z(1), at_z(3)
    x_peer = (sims, ((1 - x) * 4 + z) * 4 + y)
    flip1 = sims + 1 - 2 * lax.rem(sims, 2)
    flip2 = lax.rem(sims + 2, 4)
    core, x_near = (flip1, ell), (flip2, ell)

    def aligned(v, m):
        return pl.multiple_of(v, m)

    def z_rows(d):
        return pl.ds(aligned(ring(z, d) * group, 8), group)

    def start(kind, c, src, dst, device):
        copy = pltpu.make_async_remote_copy(
            src, dst, send.at[kind, lax.rem(c, SLOTS)], recv.at[kind, c],
            device_id=device, device_id_type=pl.DeviceIdType.MESH)

        @pl.when(c >= SLOTS)
        def _():
            copy.wait_send()

        copy.start()

    def arrived(kind, c, ref):
        pltpu.make_async_copy(ref, ref, recv.at[kind, c]).wait()

    def start_p(kind, p, src, dst, device):
        pltpu.make_async_remote_copy(
            src, dst, p_send.at[kind, p], p_recv.at[kind, p],
            device_id=device, device_id_type=pl.DeviceIdType.MESH).start()

    def arrived_p(kind, p, ref):
        pltpu.make_async_copy(ref, ref, p_recv.at[kind, p]).wait()

    def sent_p(kind, p, ref):
        pltpu.make_async_copy(ref, ref, p_send.at[kind, p]).wait()

    def where(c):
        p = lax.div(c, per)
        h = c - p * per
        return p, h, pl.ds(aligned(h * WIDTH, WIDTH), WIDTH)

    q0 = aligned(sims * quarter, 8)
    mine = pl.ds(q0, quarter)
    low_rows = pl.ds(q0, eighth)
    high_rows = pl.ds(aligned(q0 + eighth, 8), eighth)
    near_rows = pl.ds(aligned(flip2 * quarter, 8), quarter)
    core_rows = pl.ds(aligned(flip1 * quarter, 8), quarter)
    last_rows = pl.ds(aligned(lax.rem(flip1 + 2, 4) * quarter, 8), quarter)
    others = pl.ds(1, 3)

    def stage_send(c):
        p, h, cols = where(c)

        def source(rows, d):
            return tables.at[p, rows, pl.ds(aligned(ring(y, d) * span + h * WIDTH, WIDTH), WIDTH)]

        start(2, c, source(low_rows, 2), relay.at[0, c], y_up)
        start(3, c, source(high_rows, 2), relay.at[1, c], y_down)
        start(0, c, source(mine, 1), tbl.at[p, 1, mine, cols], y_up)
        start(1, c, source(mine, 3), tbl.at[p, 2, mine, cols], y_down)

    def stage_relay(c):
        p, h, cols = where(c)
        arrived(2, c, relay.at[0, c])
        start(4, c, relay.at[0, c], tbl.at[p, 3, low_rows, cols], y_up)
        arrived(3, c, relay.at[1, c])
        start(5, c, relay.at[1, c], tbl.at[p, 3, high_rows, cols], y_down)

    def stage_share(c):
        p, h, cols = where(c)
        arrived(0, c, tbl.at[p, 1, mine, cols])
        arrived(1, c, tbl.at[p, 2, mine, cols])
        arrived(4, c, tbl.at[p, 3, low_rows, cols])
        arrived(5, c, tbl.at[p, 3, high_rows, cols])
        block = tbl.at[p, others, mine, cols]
        start(6, c, block, block, x_near)
        start(7, c, block, block, core)

    def stage_pass_on(c):
        p, h, cols = where(c)
        block = tbl.at[p, others, near_rows, cols]
        arrived(6, c, block)
        start(8, c, block, block, core)

    def stage_corr(c):
        p, h, cols = where(c)
        arrived(7, c, tbl.at[p, others, core_rows, cols])
        arrived(8, c, tbl.at[p, others, last_rows, cols])

        @pl.when(h == 0)
        def _():
            pltpu.make_async_copy(tbl.at[p, 0], tbl.at[p, 0], own_sem.at[0, p]).wait()
            pltpu.make_async_copy(coef.at[p, 0], coef.at[p, 0], own_sem.at[1, p]).wait()
            arrived_p(6, p, coef.at[p, 3, pl.ds(0, half_s)])
            arrived_p(7, p, coef.at[p, 3, pl.ds(half_s, half_s)])

        total = dot3(split(coef[p, 0]), split(tbl[p, 0, :, cols]), ((1,), (0,)))
        for r in range(1, 4):
            total += dot3(split(coef[p, r]), split(tbl[p, r, :, cols]), ((1,), (0,)))
        corr[c] = total
        far = z_rows(2)
        start(9, c, corr.at[c, far, pl.ds(0, half_w)], near.at[c, 0], z_up)
        start(10, c, corr.at[c, far, pl.ds(half_w, half_w)], near.at[c, 1], z_down)

    def stage_fold(c):
        up, down = z_rows(1), z_rows(3)
        arrived(9, c, near.at[c, 0])
        corr[c, up, pl.ds(0, half_w)] += near[c, 0]
        start(11, c, corr.at[c, up], part.at[c, 0], z_up)
        arrived(10, c, near.at[c, 1])
        corr[c, down, pl.ds(half_w, half_w)] += near[c, 1]
        start(12, c, corr.at[c, down], part.at[c, 1], z_down)

    def stage_total(c):
        arrived(11, c, part.at[c, 0])
        arrived(12, c, part.at[c, 1])
        tot[c] = corr[c, z_rows(0)] + (part[c, 0] + part[c, 1])
        start(13, c, tot.at[c], other.at[c], x_peer)

    def stage_scale(c):
        p, h, cols = where(c)
        arrived(13, c, other.at[c])
        row = pl.ds(y * per + h, 1)
        factor = weights[row, :] * apod[row, :] * inv_mask[row, :]
        rows = z_rows(0)
        fixed[c, rows] = (tot[c] + other[c]) * factor
        start(14, c, fixed.at[c, rows], fixed.at[c, rows], z_up)
        start(15, c, fixed.at[c, rows], fixed.at[c, rows], z_down)

    def stage_spread(c):
        below = fixed.at[c, z_rows(3), pl.ds(0, half_w)]
        above = fixed.at[c, z_rows(1), pl.ds(half_w, half_w)]
        arrived(14, c, fixed.at[c, z_rows(3)])
        start(16, c, below, below, z_up)
        arrived(15, c, fixed.at[c, z_rows(1)])
        start(17, c, above, above, z_down)

    def stage_back(c):
        p, h, cols = where(c)
        arrived(16, c, fixed.at[c, z_rows(2), pl.ds(0, half_w)])
        arrived(17, c, fixed.at[c, z_rows(2), pl.ds(half_w, half_w)])
        values = split(fixed[c])
        for r in range(4):
            back[p, r] += dot3(split(tbl[p, r, :, cols]), values, ((1,), (1,)))

    top, bottom = pl.ds(0, half_d), pl.ds(half_d, half_d)

    def ends(c):
        p = lax.div(c, per)
        return p, c - p * per == per - 1

    def stage_ret(c):
        p, last = ends(c)

        @pl.when(last)
        def _():
            start_p(0, p, back.at[p, 3, top], ret1.at[p, 0], y_up)
            start_p(1, p, back.at[p, 3, bottom], ret1.at[p, 1], y_down)

    def stage_ret_fold(c):
        p, last = ends(c)

        @pl.when(last)
        def _():
            arrived_p(0, p, ret1.at[p, 0])
            back[p, 2, top] += ret1[p, 0]
            start_p(2, p, back.at[p, 2], ret2.at[p, 0], y_up)
            arrived_p(1, p, ret1.at[p, 1])
            back[p, 1, bottom] += ret1[p, 1]
            start_p(3, p, back.at[p, 1], ret2.at[p, 1], y_down)

    def stage_ret_sum(c):
        p, last = ends(c)

        @pl.when(last)
        def _():
            arrived_p(2, p, ret2.at[p, 0])
            arrived_p(3, p, ret2.at[p, 1])
            back[p, 0] += ret2[p, 0] + ret2[p, 1]

    def coef_send(p):
        start_p(4, p, spec.at[p], coef.at[p, 1], y_up)
        start_p(5, p, spec.at[p], coef.at[p, 2], y_down)

    def coef_relay(p):
        first, second = pl.ds(0, half_s), pl.ds(half_s, half_s)
        arrived_p(4, p, coef.at[p, 1])
        start_p(6, p, coef.at[p, 1, first], coef.at[p, 3, first], y_up)
        arrived_p(5, p, coef.at[p, 2])
        start_p(7, p, coef.at[p, 2, second], coef.at[p, 3, second], y_down)

    for p in range(3):
        pltpu.make_async_copy(
            tables.at[p, :, pl.ds(aligned(y * span, WIDTH), span)], tbl.at[p, 0], own_sem.at[0, p]).start()
        pltpu.make_async_copy(spec.at[p], coef.at[p, 0], own_sem.at[1, p]).start()

    peers = (y_up, y_down, z_up, z_down, x_peer, x_near, core)
    barrier = pltpu.get_barrier_semaphore()
    for peer in peers:
        pl.semaphore_signal(barrier, inc=1, device_id=peer, device_id_type=pl.DeviceIdType.MESH)
    pl.semaphore_wait(barrier, len(peers))

    coef_send(0)
    stage_send(0)
    back[...] = jnp.zeros_like(back)
    coef_relay(0)

    stages = dict(relay=stage_relay, share=stage_share, pass_on=stage_pass_on,
                  fold=stage_fold, total=stage_total, scale=stage_scale, spread=stage_spread,
                  corr=stage_corr, back=stage_back, ret=stage_ret,
                  ret_fold=stage_ret_fold, ret_sum=stage_ret_sum)

    def tick(t, carry):
        @pl.when(t < chunks - 1)
        def _():
            stage_send(t + 1)

        for p in (1, 2):
            @pl.when(t == p * per - 4)
            def _():
                coef_send(p)

            @pl.when(t == p * per - 2)
            def _():
                coef_relay(p)

        for name, stage in stages.items():
            c = t - (DELAY[name] - 1)

            @pl.when((c >= 0) & (c < chunks))
            def _():
                stage(c)

        return carry

    lax.fori_loop(0, chunks + DELAY["ret_sum"] - 1, tick, 0)

    out[0] = back[0, 0]
    out[1] = 0.5 * (back[1, 0] + back[2, 0])
    out[2] = 0.5 * (back[1, 0] - back[2, 0])

    def drain(i, carry):
        def sent(kind, ref):
            pltpu.make_async_copy(ref, ref, send.at[kind, i]).wait()

        quarter_block = tbl.at[0, 0, pl.ds(0, quarter), pl.ds(0, WIDTH)]
        eighth_block = tbl.at[0, 0, pl.ds(0, eighth), pl.ds(0, WIDTH)]
        three_blocks = tbl.at[0, others, pl.ds(0, quarter), pl.ds(0, WIDTH)]
        group_block = fixed.at[0, pl.ds(0, group)]
        half_block = fixed.at[0, pl.ds(0, group), pl.ds(0, half_w)]
        shapes = ([quarter_block] * 2 + [eighth_block] * 4 + [three_blocks] * 3
                  + [half_block] * 2 + [group_block] * 5 + [half_block] * 2)
        for kind, ref in enumerate(shapes):
            sent(kind, ref)
        return carry

    lax.fori_loop(0, SLOTS, drain, 0)

    def drain_p(p, carry):
        sent_p(0, p, ret1.at[p, 0])
        sent_p(1, p, ret1.at[p, 1])
        sent_p(2, p, ret2.at[p, 0])
        sent_p(3, p, ret2.at[p, 1])
        sent_p(4, p, coef.at[p, 1])
        sent_p(5, p, coef.at[p, 2])
        sent_p(6, p, coef.at[p, 3, pl.ds(0, half_s)])
        sent_p(7, p, coef.at[p, 3, pl.ds(half_s, half_s)])
        return carry

    lax.fori_loop(0, 3, drain_p, 0)


def local(spectra, tables, apodization, inv_mask, weights):
    _, depth, angles = tables.shape
    nsim = spectra.shape[2]
    span, group = angles // 4, nsim // 4
    chunks = 3 * span // WIDTH
    combined = jnp.stack([spectra[0], spectra[1] + spectra[2], spectra[1] - spectra[2]])
    turned = jnp.swapaxes(combined, 1, 2)
    rows = [v.reshape(-1, WIDTH) for v in (weights, apodization, inv_mask)]
    vmem = pl.BlockSpec(memory_space=pltpu.VMEM)
    hbm = pl.BlockSpec(memory_space=pl.ANY)

    def buffer(*shape):
        return pltpu.VMEM(shape, F32)

    return pl.pallas_call(
        kernel,
        out_shape=jax.ShapeDtypeStruct(spectra.shape, F32),
        in_specs=[hbm, hbm, vmem, vmem, vmem],
        out_specs=vmem,
        scratch_shapes=[
            buffer(3, 4, depth, span),
            buffer(2, chunks, depth // 8, WIDTH),
            buffer(3, 4, nsim, depth),
            buffer(chunks, nsim, WIDTH),
            buffer(chunks, 2, group, WIDTH // 2),
            buffer(chunks, 2, group, WIDTH),
            buffer(chunks, group, WIDTH),
            buffer(chunks, group, WIDTH),
            buffer(chunks, nsim, WIDTH),
            buffer(3, 4, depth, nsim),
            buffer(3, 2, depth // 2, nsim),
            buffer(3, 2, depth, nsim),
            pltpu.SemaphoreType.DMA((2, 3)),
            pltpu.SemaphoreType.DMA((18, SLOTS)),
            pltpu.SemaphoreType.DMA((18, chunks)),
            pltpu.SemaphoreType.DMA((8, 3)),
            pltpu.SemaphoreType.DMA((8, 3)),
        ],
        compiler_params=pltpu.CompilerParams(
            collective_id=0, has_side_effects=True, vmem_limit_bytes=60 * 1024 * 1024),
    )(turned, tables, *rows)


def solution(mesh):
    placed = (P(None, "ell", "sims"), P(None, "ell", None), P(), P(), P())
    return jax.shard_map(
        local, mesh=mesh, in_specs=placed, out_specs=P(None, "ell", "sims"), check_vma=False
    )
```

time: 490 us -> 169 us (0.34)
  waiting for transfers between devices: 433 us -> 0 us
  Pallas kernels: 0 us -> 160 us
  matrix products: 42.2 us -> 0 us
  between operations: 13.5 us -> 0.05 us
  local copies, waits for them, and re-layouts: 0.02 us -> 7.47 us
    psum x1 -> x0, waiting for transfers between devices: 433 us -> none  [local(): total = lax.psum(partial_corr, 'ell')]
    pallas_call x0 -> x1, Pallas kernels: none -> 160 us  [local(): pl.pallas_call(kernel, out_shape=jax.ShapeDtypeStruct(spectra.shape, F32)...]
    dot_general x2 -> x0, matrix products: 42.2 us -> none  [the longest x1 23 us: local(): back = jnp.einsum('pla,aps->pls', tables, fixed, precision=highest)]
  transfers between devices with their start and end apart: 1 -> 0, of which waited for: 1 -> 0; matrix products, arithmetic and copies ran while one was open for 0% -> 0% of each run, Pallas kernels for 0% -> 0%
where the time goes in v1:
time: 169 us; the launch traced here: 168 us
  Pallas kernels  160 us (95%)
  local copies, waits for them, and re-layouts  7.47 us (4%)
    pallas_call x1, Pallas kernels, local(): pl.pallas_call(kernel, out_shape=jax.ShapeDtypeStruct(spectra.shape, F32)...  160 us
    reshape x3, local copies, waits for them, and re-layouts, local(): rows = [v.reshape(-1, WIDTH) for v in (weights, apodization, inv_mask)]  4.04 us

profile of v1, /device:TPU:0, one launch (start us, length us, event | category | flops | bytes accessed | tf_op | source)
XLA Modules:
  0.0 168.0 jit_solution(14361596744674043135)
XLA Ops:
  0.0 1.2 fusion
  1.2 0.1 copy.10
  1.3 0.1 copy.11
  1.5 0.1 copy.9
  1.6 0.9 maximum_bitcast_fusion.spec
  2.5 1.3 reshape.10.apod
  3.8 1.3 reshape.11.inv_mask
  5.2 1.4 reshape.9.weights
  6.5 159.5 %shard_map.55 = f32[3,192,224]{2,1,0:T(8,128)} custom-call(f32[3,224,192]{2,1,0:T(8,128)} %maximum_bitcast_fusion.spec, f32[3,192,6144]{2,1,0:T(8,128)} %tables.1, f32[24,256]{1,0:T(8,128)} %reshape.9.weights, f32[24,256]{1,0:T(8,128)} %reshape.10.apod, f32[24,256]{1,0:T(8,128)} %reshape.11.inv_mask), custom_call_target="tpu_custom_call" | custom-call | tf_op jit(solution)/shard_map/pallas_call | solution.py:335
  166.0 1.9 %copy.13 = f32[3,192,224]{2,1,0:T(8,128)} copy(f32[3,192,224]{2,1,0:T(8,128)} %shard_map.55) | data formatting | bytes 1032192
  (1 shorter events, 0.0 us)

commit v2 on v1

--- a/solution.py
+++ b/solution.py
@@ -7,8 +7,11 @@
 
 WIDTH = 256
 SLOTS = 4
-DELAY = dict(relay=1, share=2, pass_on=3, corr=4, fold=5, total=6, scale=7,
-             spread=8, back=9, ret=10, ret_fold=11, ret_sum=12)
+ORDER = ("back", "corr", "fold", "relay", "ret", "pass_on", "ret_fold", "ret_sum", "total",
+         "spread", "scale", "share", "send")
+LEAD, FIRST = 2, 1
+DELAY = dict(send=-LEAD, relay=0, share=1, pass_on=3, corr=4, fold=5, total=6, scale=8,
+             spread=10, back=13, ret=13, ret_fold=15, ret_sum=17)
 F32, BF16 = jnp.float32, jnp.bfloat16
 
 
@@ -24,8 +27,8 @@
     return dot(a[0], b[0]) + (dot(a[0], b[1]) + dot(a[1], b[0]))
 
 
-def kernel(spec, tables, weights, apod, inv_mask, out, tbl, relay, coef, corr, near,
-           part, other, tot, fixed, back, ret1, ret2, own_sem, send, recv, p_send, p_recv):
+def kernel(spec, tables, weights, apod, inv_mask, out, tbl, relay, coef, coef_hi, coef_lo, corr,
+           near, part, other, tot, fixed, back, ret1, ret2, own_sem, send, recv, p_send, p_recv):
     sims, ell = lax.axis_index("sims"), lax.axis_index("ell")
     y, z, x = lax.rem(ell, 4), lax.rem(lax.div(ell, 4), 4), lax.div(ell, 16)
     depth, nsim = out.shape[1], out.shape[2]
@@ -34,7 +37,7 @@
     chunks = 3 * per
     quarter, eighth = depth // 4, depth // 8
     group = nsim // 4
-    half_w, half_d, half_s = WIDTH // 2, depth // 2, nsim // 2
+    half_w, half_d = WIDTH // 2, depth // 2
 
     def ring(v, d):
         return lax.rem(v + d, 4)
@@ -95,6 +98,7 @@
     core_rows = pl.ds(aligned(flip1 * quarter, 8), quarter)
     last_rows = pl.ds(aligned(lax.rem(flip1 + 2, 4) * quarter, 8), quarter)
     others = pl.ds(1, 3)
+    top, bottom = pl.ds(0, half_d), pl.ds(half_d, half_d)
 
     def stage_send(c):
         p, h, cols = where(c)
@@ -138,13 +142,14 @@
         @pl.when(h == 0)
         def _():
             pltpu.make_async_copy(tbl.at[p, 0], tbl.at[p, 0], own_sem.at[0, p]).wait()
-            pltpu.make_async_copy(coef.at[p, 0], coef.at[p, 0], own_sem.at[1, p]).wait()
-            arrived_p(6, p, coef.at[p, 3, pl.ds(0, half_s)])
-            arrived_p(7, p, coef.at[p, 3, pl.ds(half_s, half_s)])
-
-        total = dot3(split(coef[p, 0]), split(tbl[p, 0, :, cols]), ((1,), (0,)))
+            arrived_p(6, p, coef.at[p, 3, top])
+            arrived_p(7, p, coef.at[p, 3, bottom])
+            for r in range(4):
+                coef_hi[r], coef_lo[r] = split(coef[p, r].T)
+
+        total = dot3((coef_hi[0], coef_lo[0]), split(tbl[p, 0, :, cols]), ((1,), (0,)))
         for r in range(1, 4):
-            total += dot3(split(coef[p, r]), split(tbl[p, r, :, cols]), ((1,), (0,)))
+            total += dot3((coef_hi[r], coef_lo[r]), split(tbl[p, r, :, cols]), ((1,), (0,)))
         corr[c] = total
         far = z_rows(2)
         start(9, c, corr.at[c, far, pl.ds(0, half_w)], near.at[c, 0], z_up)
@@ -168,8 +173,8 @@
     def stage_scale(c):
         p, h, cols = where(c)
         arrived(13, c, other.at[c])
-        row = pl.ds(y * per + h, 1)
-        factor = weights[row, :] * apod[row, :] * inv_mask[row, :]
+        here = pl.ds(aligned(y * span + h * WIDTH, WIDTH), WIDTH)
+        factor = weights[:, here] * apod[:, here] * inv_mask[:, here]
         rows = z_rows(0)
         fixed[c, rows] = (tot[c] + other[c]) * factor
         start(14, c, fixed.at[c, rows], fixed.at[c, rows], z_up)
@@ -191,8 +196,6 @@
         for r in range(4):
             back[p, r] += dot3(split(tbl[p, r, :, cols]), values, ((1,), (1,)))
 
-    top, bottom = pl.ds(0, half_d), pl.ds(half_d, half_d)
-
     def ends(c):
         p = lax.div(c, per)
         return p, c - p * per == per - 1
@@ -227,15 +230,15 @@
             back[p, 0] += ret2[p, 0] + ret2[p, 1]
 
     def coef_send(p):
-        start_p(4, p, spec.at[p], coef.at[p, 1], y_up)
-        start_p(5, p, spec.at[p], coef.at[p, 2], y_down)
+        source = spec.at[0] if p == 0 else coef.at[p, 0]
+        start_p(4, p, source, coef.at[p, 1], y_up)
+        start_p(5, p, source, coef.at[p, 2], y_down)
 
     def coef_relay(p):
-        first, second = pl.ds(0, half_s), pl.ds(half_s, half_s)
         arrived_p(4, p, coef.at[p, 1])
-        start_p(6, p, coef.at[p, 1, first], coef.at[p, 3, first], y_up)
+        start_p(6, p, coef.at[p, 1, top], coef.at[p, 3, top], y_up)
         arrived_p(5, p, coef.at[p, 2])
-        start_p(7, p, coef.at[p, 2, second], coef.at[p, 3, second], y_down)
+        start_p(7, p, coef.at[p, 2, bottom], coef.at[p, 3, bottom], y_down)
 
     for p in range(3):
         pltpu.make_async_copy(
@@ -248,40 +251,44 @@
         pl.semaphore_signal(barrier, inc=1, device_id=peer, device_id_type=pl.DeviceIdType.MESH)
     pl.semaphore_wait(barrier, len(peers))
 
+    stage_send(0)
     coef_send(0)
-    stage_send(0)
+    for c in range(1, LEAD):
+        stage_send(c)
+    for p in range(3):
+        pltpu.make_async_copy(coef.at[p, 0], coef.at[p, 0], own_sem.at[1, p]).wait()
+    ee, bb = coef[1, 0], coef[2, 0]
+    coef[1, 0] = ee + bb
+    coef[2, 0] = ee - bb
     back[...] = jnp.zeros_like(back)
-    coef_relay(0)
-
-    stages = dict(relay=stage_relay, share=stage_share, pass_on=stage_pass_on,
+
+    stages = dict(send=stage_send, relay=stage_relay, share=stage_share, pass_on=stage_pass_on,
                   fold=stage_fold, total=stage_total, scale=stage_scale, spread=stage_spread,
                   corr=stage_corr, back=stage_back, ret=stage_ret,
                   ret_fold=stage_ret_fold, ret_sum=stage_ret_sum)
 
     def tick(t, carry):
-        @pl.when(t < chunks - 1)
-        def _():
-            stage_send(t + 1)
-
-        for p in (1, 2):
-            @pl.when(t == p * per - 4)
+        for name in ORDER:
+            c = t - DELAY[name]
+
+            @pl.when((c >= 0 if name != "send" else c >= LEAD) & (c < chunks))
             def _():
-                coef_send(p)
-
-            @pl.when(t == p * per - 2)
-            def _():
-                coef_relay(p)
-
-        for name, stage in stages.items():
-            c = t - (DELAY[name] - 1)
-
-            @pl.when((c >= 0) & (c < chunks))
-            def _():
-                stage(c)
+                stages[name](c)
+
+            if name == "send":
+                for p in range(3):
+                    if p:
+                        @pl.when(t == p * per - 4)
+                        def _():
+                            coef_send(p)
+
+                    @pl.when(t == (p * per - 2 if p else FIRST))
+                    def _():
+                        coef_relay(p)
 
         return carry
 
-    lax.fori_loop(0, chunks + DELAY["ret_sum"] - 1, tick, 0)
+    lax.fori_loop(0, chunks + max(DELAY.values()), tick, 0)
 
     out[0] = back[0, 0]
     out[1] = 0.5 * (back[1, 0] + back[2, 0])
@@ -311,8 +318,8 @@
         sent_p(3, p, ret2.at[p, 1])
         sent_p(4, p, coef.at[p, 1])
         sent_p(5, p, coef.at[p, 2])
-        sent_p(6, p, coef.at[p, 3, pl.ds(0, half_s)])
-        sent_p(7, p, coef.at[p, 3, pl.ds(half_s, half_s)])
+        sent_p(6, p, coef.at[p, 3, top])
+        sent_p(7, p, coef.at[p, 3, bottom])
         return carry
 
     lax.fori_loop(0, 3, drain_p, 0)
@@ -323,9 +330,7 @@
     nsim = spectra.shape[2]
     span, group = angles // 4, nsim // 4
     chunks = 3 * span // WIDTH
-    combined = jnp.stack([spectra[0], spectra[1] + spectra[2], spectra[1] - spectra[2]])
-    turned = jnp.swapaxes(combined, 1, 2)
-    rows = [v.reshape(-1, WIDTH) for v in (weights, apodization, inv_mask)]
+    rows = [v.reshape(1, -1) for v in (weights, apodization, inv_mask)]
     vmem = pl.BlockSpec(memory_space=pltpu.VMEM)
     hbm = pl.BlockSpec(memory_space=pl.ANY)
 
@@ -340,7 +345,9 @@
         scratch_shapes=[
             buffer(3, 4, depth, span),
             buffer(2, chunks, depth // 8, WIDTH),
-            buffer(3, 4, nsim, depth),
+            buffer(3, 4, depth, nsim),
+            pltpu.VMEM((4, nsim, depth), BF16),
+            pltpu.VMEM((4, nsim, depth), BF16),
             buffer(chunks, nsim, WIDTH),
             buffer(chunks, 2, group, WIDTH // 2),
             buffer(chunks, 2, group, WIDTH),
@@ -358,7 +365,7 @@
         ],
         compiler_params=pltpu.CompilerParams(
             collective_id=0, has_side_effects=True, vmem_limit_bytes=60 * 1024 * 1024),
-    )(turned, tables, *rows)
+    )(spectra, tables, *rows)
 
 
 def solution(mesh):

time: 169 us -> 135 us (0.80)
  Pallas kernels: 160 us -> 133 us
  local copies, waits for them, and re-layouts: 7.47 us -> 1.92 us
    pallas_call x1, Pallas kernels: 160 us -> 133 us  [local(): pl.pallas_call(kernel, out_shape=jax.ShapeDtypeStruct(spectra.shape, F32)...]
    reshape x3 -> x0, local copies, waits for them, and re-layouts: 4.04 us -> none  [local(): rows = [v.reshape(-1, WIDTH) for v in (weights, apodization, inv_mask)]]
where the time goes in v2:
time: 135 us
  Pallas kernels  133 us (99%)
  local copies, waits for them, and re-layouts  1.92 us (1%)
    pallas_call x1, Pallas kernels, local(): pl.pallas_call(kernel, out_shape=jax.ShapeDtypeStruct(spectra.shape, F32)...  133 us

profile of v2, /device:TPU:0, one launch (start us, length us, event | category | flops | bytes accessed | tf_op | source)
XLA Modules:
  0.0 134.8 jit_solution(7919167556511916169)
XLA Ops:
  0.0 132.9 %shard_map.55 = f32[3,192,224]{2,1,0:T(8,128)} custom-call(f32[3,192,224]{2,1,0:T(8,128)} %spec.1, f32[3,192,6144]{2,1,0:T(8,128)} %tables.1, f32[1,6144]{1,0:T(1,128)} %bitcast.3, f32[1,6144]{1,0:T(1,128)} %bitcast.4, f32[1,6144]{1,0:T(1,128)} %bitcast.5), custom_call_target="tpu_custom_call" | custom-call | tf_op jit(solution)/shard_map/pallas_call | solution.py:340
  132.9 1.9 %copy.7 = f32[3,192,224]{2,1,0:T(8,128)} copy(f32[3,192,224]{2,1,0:T(8,128)} %shard_map.55) | data formatting | bytes 1032192

commit v3 on v2

--- a/solution.py
+++ b/solution.py
@@ -7,11 +7,15 @@
 
 WIDTH = 256
 SLOTS = 4
-ORDER = ("back", "corr", "fold", "relay", "ret", "pass_on", "ret_fold", "ret_sum", "total",
-         "spread", "scale", "share", "send")
-LEAD, FIRST = 2, 1
-DELAY = dict(send=-LEAD, relay=0, share=1, pass_on=3, corr=4, fold=5, total=6, scale=8,
-             spread=10, back=13, ret=13, ret_fold=15, ret_sum=17)
+ORDER = (
+    "share", "back", "cross", "spread", "corr", "ret_fold", "fold", "total", "relay",
+    "ret_sum", "pass_on", "ret", "send", "scale",
+)
+LEAD, FIRST, DIRECT = 2, 1, 3
+DELAY = dict(
+    relay=0, share=2, pass_on=3, corr=4, fold=5, total=6, cross=8, scale=9, spread=11,
+    back=13, ret=13, ret_fold=15, ret_sum=17, send=-2,
+)
 F32, BF16 = jnp.float32, jnp.bfloat16
 
 
@@ -28,14 +32,14 @@
 
 
 def kernel(spec, tables, weights, apod, inv_mask, out, tbl, relay, coef, coef_hi, coef_lo, corr,
-           near, part, other, tot, fixed, back, ret1, ret2, own_sem, send, recv, p_send, p_recv):
+           near, part, cross, other, tot, fixed, back, ret1, ret2, own_sem, send, recv, p_send, p_recv):
     sims, ell = lax.axis_index("sims"), lax.axis_index("ell")
     y, z, x = lax.rem(ell, 4), lax.rem(lax.div(ell, 4), 4), lax.div(ell, 16)
     depth, nsim = out.shape[1], out.shape[2]
     span = tbl.shape[3]
     per = span // WIDTH
     chunks = 3 * per
-    quarter, eighth = depth // 4, depth // 8
+    quarter = depth // 4
     group = nsim // 4
     half_w, half_d = WIDTH // 2, depth // 2
 
@@ -49,10 +53,10 @@
         return (sims, (x * 4 + ring(z, d)) * 4 + y)
 
     y_up, y_down, z_up, z_down = at_y(1), at_y(3), at_z(1), at_z(3)
-    x_peer = (sims, ((1 - x) * 4 + z) * 4 + y)
     flip1 = sims + 1 - 2 * lax.rem(sims, 2)
     flip2 = lax.rem(sims + 2, 4)
     core, x_near = (flip1, ell), (flip2, ell)
+    x_far = (flip2, ((1 - x) * 4 + z) * 4 + y)
 
     def aligned(v, m):
         return pl.multiple_of(v, m)
@@ -91,14 +95,30 @@
         return p, h, pl.ds(aligned(h * WIDTH, WIDTH), WIDTH)
 
     q0 = aligned(sims * quarter, 8)
-    mine = pl.ds(q0, quarter)
-    low_rows = pl.ds(q0, eighth)
-    high_rows = pl.ds(aligned(q0 + eighth, 8), eighth)
     near_rows = pl.ds(aligned(flip2 * quarter, 8), quarter)
     core_rows = pl.ds(aligned(flip1 * quarter, 8), quarter)
     last_rows = pl.ds(aligned(lax.rem(flip1 + 2, 4) * quarter, 8), quarter)
     others = pl.ds(1, 3)
+    left, right = pl.ds(0, half_w), pl.ds(half_w, half_w)
     top, bottom = pl.ds(0, half_d), pl.ds(half_d, half_d)
+
+    def by_kind(c, run):
+        direct = lax.rem(c, SLOTS) == DIRECT
+
+        @pl.when(direct)
+        def _():
+            run(True)
+
+        @pl.when(jnp.logical_not(direct))
+        def _():
+            run(False)
+
+    def rows_for(direct):
+        count = depth // 2 if direct else quarter
+        base = aligned(lax.rem(sims, 2) * count, 8) if direct else q0
+        half = count // 2
+        return (pl.ds(base, count), pl.ds(base, half),
+                pl.ds(aligned(base + half, 8), half), pl.ds(0, half))
 
     def stage_send(c):
         p, h, cols = where(c)
@@ -106,38 +126,64 @@
         def source(rows, d):
             return tables.at[p, rows, pl.ds(aligned(ring(y, d) * span + h * WIDTH, WIDTH), WIDTH)]
 
-        start(2, c, source(low_rows, 2), relay.at[0, c], y_up)
-        start(3, c, source(high_rows, 2), relay.at[1, c], y_down)
-        start(0, c, source(mine, 1), tbl.at[p, 1, mine, cols], y_up)
-        start(1, c, source(mine, 3), tbl.at[p, 2, mine, cols], y_down)
+        def run(direct):
+            rows, low, high, held = rows_for(direct)
+            start(2, c, source(low, 2), relay.at[0, c, held], y_up)
+            start(3, c, source(high, 2), relay.at[1, c, held], y_down)
+            start(0, c, source(rows, 1), tbl.at[p, 1, rows, cols], y_up)
+            start(1, c, source(rows, 3), tbl.at[p, 2, rows, cols], y_down)
+
+        by_kind(c, run)
 
     def stage_relay(c):
         p, h, cols = where(c)
-        arrived(2, c, relay.at[0, c])
-        start(4, c, relay.at[0, c], tbl.at[p, 3, low_rows, cols], y_up)
-        arrived(3, c, relay.at[1, c])
-        start(5, c, relay.at[1, c], tbl.at[p, 3, high_rows, cols], y_down)
+
+        def run(direct):
+            rows, low, high, held = rows_for(direct)
+            arrived(2, c, relay.at[0, c, held])
+            start(4, c, relay.at[0, c, held], tbl.at[p, 3, low, cols], y_up)
+            arrived(3, c, relay.at[1, c, held])
+            start(5, c, relay.at[1, c, held], tbl.at[p, 3, high, cols], y_down)
+
+        by_kind(c, run)
 
     def stage_share(c):
         p, h, cols = where(c)
-        arrived(0, c, tbl.at[p, 1, mine, cols])
-        arrived(1, c, tbl.at[p, 2, mine, cols])
-        arrived(4, c, tbl.at[p, 3, low_rows, cols])
-        arrived(5, c, tbl.at[p, 3, high_rows, cols])
-        block = tbl.at[p, others, mine, cols]
-        start(6, c, block, block, x_near)
-        start(7, c, block, block, core)
+
+        def run(direct):
+            rows, low, high, held = rows_for(direct)
+            arrived(0, c, tbl.at[p, 1, rows, cols])
+            arrived(1, c, tbl.at[p, 2, rows, cols])
+            arrived(4, c, tbl.at[p, 3, low, cols])
+            arrived(5, c, tbl.at[p, 3, high, cols])
+            block = tbl.at[p, others, rows, cols]
+            if not direct:
+                start(6, c, block, block, x_near)
+            start(7, c, block, block, core)
+
+        by_kind(c, run)
 
     def stage_pass_on(c):
         p, h, cols = where(c)
-        block = tbl.at[p, others, near_rows, cols]
-        arrived(6, c, block)
-        start(8, c, block, block, core)
+
+        @pl.when(lax.rem(c, SLOTS) != DIRECT)
+        def _():
+            block = tbl.at[p, others, near_rows, cols]
+            arrived(6, c, block)
+            start(8, c, block, block, core)
 
     def stage_corr(c):
         p, h, cols = where(c)
-        arrived(7, c, tbl.at[p, others, core_rows, cols])
-        arrived(8, c, tbl.at[p, others, last_rows, cols])
+
+        def run(direct):
+            if direct:
+                half = pl.ds(aligned(lax.rem(flip1, 2) * half_d, 8), half_d)
+                arrived(7, c, tbl.at[p, others, half, cols])
+            else:
+                arrived(7, c, tbl.at[p, others, core_rows, cols])
+                arrived(8, c, tbl.at[p, others, last_rows, cols])
+
+        by_kind(c, run)
 
         @pl.when(h == 0)
         def _():
@@ -168,11 +214,19 @@
         arrived(11, c, part.at[c, 0])
         arrived(12, c, part.at[c, 1])
         tot[c] = corr[c, z_rows(0)] + (part[c, 0] + part[c, 1])
-        start(13, c, tot.at[c], other.at[c], x_peer)
+        start(13, c, tot.at[c, :, left], cross.at[c, 0], x_near)
+        start(18, c, tot.at[c, :, right], cross.at[c, 1], x_far)
+
+    def stage_cross(c):
+        arrived(13, c, cross.at[c, 0])
+        start(19, c, cross.at[c, 0], other.at[c, :, left], x_far)
+        arrived(18, c, cross.at[c, 1])
+        start(20, c, cross.at[c, 1], other.at[c, :, right], x_near)
 
     def stage_scale(c):
         p, h, cols = where(c)
-        arrived(13, c, other.at[c])
+        arrived(19, c, other.at[c, :, left])
+        arrived(20, c, other.at[c, :, right])
         here = pl.ds(aligned(y * span + h * WIDTH, WIDTH), WIDTH)
         factor = weights[:, here] * apod[:, here] * inv_mask[:, here]
         rows = z_rows(0)
@@ -207,6 +261,8 @@
         def _():
             start_p(0, p, back.at[p, 3, top], ret1.at[p, 0], y_up)
             start_p(1, p, back.at[p, 3, bottom], ret1.at[p, 1], y_down)
+            start_p(2, p, back.at[p, 2, bottom], ret2.at[p, 0, bottom], y_up)
+            start_p(3, p, back.at[p, 1, top], ret2.at[p, 1, top], y_down)
 
     def stage_ret_fold(c):
         p, last = ends(c)
@@ -215,18 +271,20 @@
         def _():
             arrived_p(0, p, ret1.at[p, 0])
             back[p, 2, top] += ret1[p, 0]
-            start_p(2, p, back.at[p, 2], ret2.at[p, 0], y_up)
+            start_p(8, p, back.at[p, 2, top], ret2.at[p, 0, top], y_up)
             arrived_p(1, p, ret1.at[p, 1])
             back[p, 1, bottom] += ret1[p, 1]
-            start_p(3, p, back.at[p, 1], ret2.at[p, 1], y_down)
+            start_p(9, p, back.at[p, 1, bottom], ret2.at[p, 1, bottom], y_down)
 
     def stage_ret_sum(c):
         p, last = ends(c)
 
         @pl.when(last)
         def _():
-            arrived_p(2, p, ret2.at[p, 0])
-            arrived_p(3, p, ret2.at[p, 1])
+            arrived_p(2, p, ret2.at[p, 0, bottom])
+            arrived_p(3, p, ret2.at[p, 1, top])
+            arrived_p(8, p, ret2.at[p, 0, top])
+            arrived_p(9, p, ret2.at[p, 1, bottom])
             back[p, 0] += ret2[p, 0] + ret2[p, 1]
 
     def coef_send(p):
@@ -245,7 +303,7 @@
             tables.at[p, :, pl.ds(aligned(y * span, WIDTH), span)], tbl.at[p, 0], own_sem.at[0, p]).start()
         pltpu.make_async_copy(spec.at[p], coef.at[p, 0], own_sem.at[1, p]).start()
 
-    peers = (y_up, y_down, z_up, z_down, x_peer, x_near, core)
+    peers = (y_up, y_down, z_up, z_down, x_far, x_near, core)
     barrier = pltpu.get_barrier_semaphore()
     for peer in peers:
         pl.semaphore_signal(barrier, inc=1, device_id=peer, device_id_type=pl.DeviceIdType.MESH)
@@ -263,7 +321,7 @@
     back[...] = jnp.zeros_like(back)
 
     stages = dict(send=stage_send, relay=stage_relay, share=stage_share, pass_on=stage_pass_on,
-                  fold=stage_fold, total=stage_total, scale=stage_scale, spread=stage_spread,
+                  fold=stage_fold, total=stage_total, cross=stage_cross, scale=stage_scale, spread=stage_spread,
                   corr=stage_corr, back=stage_back, ret=stage_ret,
                   ret_fold=stage_ret_fold, ret_sum=stage_ret_sum)
 
@@ -294,28 +352,27 @@
     out[1] = 0.5 * (back[1, 0] + back[2, 0])
     out[2] = 0.5 * (back[1, 0] - back[2, 0])
 
-    def drain(i, carry):
-        def sent(kind, ref):
-            pltpu.make_async_copy(ref, ref, send.at[kind, i]).wait()
-
-        quarter_block = tbl.at[0, 0, pl.ds(0, quarter), pl.ds(0, WIDTH)]
-        eighth_block = tbl.at[0, 0, pl.ds(0, eighth), pl.ds(0, WIDTH)]
-        three_blocks = tbl.at[0, others, pl.ds(0, quarter), pl.ds(0, WIDTH)]
-        group_block = fixed.at[0, pl.ds(0, group)]
-        half_block = fixed.at[0, pl.ds(0, group), pl.ds(0, half_w)]
-        shapes = ([quarter_block] * 2 + [eighth_block] * 4 + [three_blocks] * 3
-                  + [half_block] * 2 + [group_block] * 5 + [half_block] * 2)
+    def block(ref, count, width=WIDTH):
+        return ref.at[0, pl.ds(0, count), pl.ds(0, width)]
+
+    for i in range(SLOTS):
+        count = depth // 2 if i == DIRECT else quarter
+        three = tbl.at[0, others, pl.ds(0, count), pl.ds(0, WIDTH)]
+        one, two = block(corr, group), block(corr, group, half_w)
+        whole, half = block(tbl.at[0], count), block(tbl.at[0], count // 2)
+        shapes = [whole] * 2 + [half] * 4 + [three] * 3 + [two] * 2 + [one] * 2
+        shapes += [two] + [one] * 2 + [two] * 5
         for kind, ref in enumerate(shapes):
-            sent(kind, ref)
-        return carry
-
-    lax.fori_loop(0, SLOTS, drain, 0)
+            if i != DIRECT or kind not in (6, 8):
+                pltpu.make_async_copy(ref, ref, send.at[kind, i]).wait()
 
     def drain_p(p, carry):
         sent_p(0, p, ret1.at[p, 0])
         sent_p(1, p, ret1.at[p, 1])
-        sent_p(2, p, ret2.at[p, 0])
-        sent_p(3, p, ret2.at[p, 1])
+        sent_p(2, p, ret2.at[p, 0, bottom])
+        sent_p(3, p, ret2.at[p, 1, top])
+        sent_p(8, p, ret2.at[p, 0, top])
+        sent_p(9, p, ret2.at[p, 1, bottom])
         sent_p(4, p, coef.at[p, 1])
         sent_p(5, p, coef.at[p, 2])
         sent_p(6, p, coef.at[p, 3, top])
@@ -344,13 +401,14 @@
         out_specs=vmem,
         scratch_shapes=[
             buffer(3, 4, depth, span),
-            buffer(2, chunks, depth // 8, WIDTH),
+            buffer(2, chunks, depth // 4, WIDTH),
             buffer(3, 4, depth, nsim),
             pltpu.VMEM((4, nsim, depth), BF16),
             pltpu.VMEM((4, nsim, depth), BF16),
             buffer(chunks, nsim, WIDTH),
             buffer(chunks, 2, group, WIDTH // 2),
             buffer(chunks, 2, group, WIDTH),
+            buffer(chunks, 2, group, WIDTH // 2),
             buffer(chunks, group, WIDTH),
             buffer(chunks, group, WIDTH),
             buffer(chunks, nsim, WIDTH),
@@ -358,10 +416,10 @@
             buffer(3, 2, depth // 2, nsim),
             buffer(3, 2, depth, nsim),
             pltpu.SemaphoreType.DMA((2, 3)),
-            pltpu.SemaphoreType.DMA((18, SLOTS)),
-            pltpu.SemaphoreType.DMA((18, chunks)),
-            pltpu.SemaphoreType.DMA((8, 3)),
-            pltpu.SemaphoreType.DMA((8, 3)),
+            pltpu.SemaphoreType.DMA((21, SLOTS)),
+            pltpu.SemaphoreType.DMA((21, chunks)),
+            pltpu.SemaphoreType.DMA((10, 3)),
+            pltpu.SemaphoreType.DMA((10, 3)),
         ],
         compiler_params=pltpu.CompilerParams(
             collective_id=0, has_side_effects=True, vmem_limit_bytes=60 * 1024 * 1024),

time: 135 us -> 130 us (0.963)
  Pallas kernels: 133 us -> 128 us
    pallas_call x1, Pallas kernels: 133 us -> 128 us  [local(): pl.pallas_call(kernel, out_shape=jax.ShapeDtypeStruct(spectra.shape, F32)...]
where the time goes in v3:
time: 130 us
  Pallas kernels  128 us (98%)
  local copies, waits for them, and re-layouts  1.92 us (1%)
    pallas_call x1, Pallas kernels, local(): pl.pallas_call(kernel, out_shape=jax.ShapeDtypeStruct(spectra.shape, F32)...  128 us

profile of v3, /device:TPU:0, one launch (start us, length us, event | category | flops | bytes accessed | tf_op | source)
XLA Modules:
  0.0 130.3 jit_solution(7200239713339892146)
XLA Ops:
  0.0 128.3 %shard_map.55 = f32[3,192,224]{2,1,0:T(8,128)} custom-call(f32[3,192,224]{2,1,0:T(8,128)} %spec.1, f32[3,192,6144]{2,1,0:T(8,128)} %tables.1, f32[1,6144]{1,0:T(1,128)} %bitcast.3, f32[1,6144]{1,0:T(1,128)} %bitcast.4, f32[1,6144]{1,0:T(1,128)} %bitcast.5), custom_call_target="tpu_custom_call" | custom-call | tf_op jit(solution)/shard_map/pallas_call | solution.py:397
  128.4 1.9 %copy.7 = f32[3,192,224]{2,1,0:T(8,128)} copy(f32[3,192,224]{2,1,0:T(8,128)} %shard_map.55) | data formatting | bytes 1032192

commit v4 on v3

--- a/solution.py
+++ b/solution.py
@@ -11,7 +11,7 @@
     "share", "back", "cross", "spread", "corr", "ret_fold", "fold", "total", "relay",
     "ret_sum", "pass_on", "ret", "send", "scale",
 )
-LEAD, FIRST, DIRECT = 2, 1, 3
+LEAD, FIRST, DIRECT, STRIP_LAG = 2, 1, 3, 2
 DELAY = dict(
     relay=0, share=2, pass_on=3, corr=4, fold=5, total=6, cross=8, scale=9, spread=11,
     back=13, ret=13, ret_fold=15, ret_sum=17, send=-2,
@@ -32,7 +32,8 @@
 
 
 def kernel(spec, tables, weights, apod, inv_mask, out, tbl, relay, coef, coef_hi, coef_lo, corr,
-           near, part, cross, other, tot, fixed, back, ret1, ret2, own_sem, send, recv, p_send, p_recv):
+           near, part, cross, other, tot, fixed, back, ret1, ret2, own_sem, send, recv, p_send, p_recv,
+           s_send, s_recv):
     sims, ell = lax.axis_index("sims"), lax.axis_index("ell")
     y, z, x = lax.rem(ell, 4), lax.rem(lax.div(ell, 4), 4), lax.div(ell, 16)
     depth, nsim = out.shape[1], out.shape[2]
@@ -188,8 +189,16 @@
         @pl.when(h == 0)
         def _():
             pltpu.make_async_copy(tbl.at[p, 0], tbl.at[p, 0], own_sem.at[0, p]).wait()
-            arrived_p(6, p, coef.at[p, 3, top])
-            arrived_p(7, p, coef.at[p, 3, bottom])
+            @pl.when(p == 0)
+            def _():
+                arrived_p(6, 0, coef.at[0, 3, top])
+                arrived_p(7, 0, coef.at[0, 3, bottom])
+
+            @pl.when(p > 0)
+            def _():
+                for k in range(per):
+                    done_s(s_recv, 2, (p - 1) * per + k, coef.at[p, 3, pl.ds(k * strip, strip)])
+
             for r in range(4):
                 coef_hi[r], coef_lo[r] = split(coef[p, r].T)
 
@@ -287,16 +296,47 @@
             arrived_p(9, p, ret2.at[p, 1, bottom])
             back[p, 0] += ret2[p, 0] + ret2[p, 1]
 
-    def coef_send(p):
-        source = spec.at[0] if p == 0 else coef.at[p, 0]
-        start_p(4, p, source, coef.at[p, 1], y_up)
-        start_p(5, p, source, coef.at[p, 2], y_down)
-
-    def coef_relay(p):
-        arrived_p(4, p, coef.at[p, 1])
-        start_p(6, p, coef.at[p, 1, top], coef.at[p, 3, top], y_up)
-        arrived_p(5, p, coef.at[p, 2])
-        start_p(7, p, coef.at[p, 2, bottom], coef.at[p, 3, bottom], y_down)
+    def coef_send():
+        start_p(4, 0, spec.at[0], coef.at[0, 1], y_up)
+        start_p(5, 0, spec.at[0], coef.at[0, 2], y_down)
+
+    def coef_relay():
+        arrived_p(4, 0, coef.at[0, 1])
+        start_p(6, 0, coef.at[0, 1, top], coef.at[0, 3, top], y_up)
+        arrived_p(5, 0, coef.at[0, 2])
+        start_p(7, 0, coef.at[0, 2, bottom], coef.at[0, 3, bottom], y_down)
+
+    strip = depth // per
+
+    def strip_of(i):
+        p, k = lax.div(i, per), lax.rem(i, per)
+        return p + 1, k, pl.ds(aligned(k * strip, 8), strip)
+
+    def start_s(kind, i, src, dst, device):
+        pltpu.make_async_remote_copy(
+            src, dst, s_send.at[kind, i], s_recv.at[kind, i],
+            device_id=device, device_id_type=pl.DeviceIdType.MESH).start()
+
+    def done_s(sems, kind, i, ref):
+        pltpu.make_async_copy(ref, ref, sems.at[kind, i]).wait()
+
+    def strip_send(i):
+        p, k, rows = strip_of(i)
+        start_s(0, i, coef.at[p, 0, rows], coef.at[p, 1, rows], y_up)
+        start_s(1, i, coef.at[p, 0, rows], coef.at[p, 2, rows], y_down)
+
+    def strip_relay(i):
+        p, k, rows = strip_of(i)
+        done_s(s_recv, 0, i, coef.at[p, 1, rows])
+        done_s(s_recv, 1, i, coef.at[p, 2, rows])
+
+        @pl.when(k < per // 2)
+        def _():
+            start_s(2, i, coef.at[p, 1, rows], coef.at[p, 3, rows], y_up)
+
+        @pl.when(k >= per // 2)
+        def _():
+            start_s(2, i, coef.at[p, 2, rows], coef.at[p, 3, rows], y_down)
 
     for p in range(3):
         pltpu.make_async_copy(
@@ -310,7 +350,7 @@
     pl.semaphore_wait(barrier, len(peers))
 
     stage_send(0)
-    coef_send(0)
+    coef_send()
     for c in range(1, LEAD):
         stage_send(c)
     for p in range(3):
@@ -334,15 +374,17 @@
                 stages[name](c)
 
             if name == "send":
-                for p in range(3):
-                    if p:
-                        @pl.when(t == p * per - 4)
-                        def _():
-                            coef_send(p)
-
-                    @pl.when(t == (p * per - 2 if p else FIRST))
-                    def _():
-                        coef_relay(p)
+                @pl.when(t == FIRST)
+                def _():
+                    coef_relay()
+
+                @pl.when(t < 2 * per)
+                def _():
+                    strip_send(t)
+
+                @pl.when((t >= STRIP_LAG) & (t < 2 * per + STRIP_LAG))
+                def _():
+                    strip_relay(t - STRIP_LAG)
 
         return carry
 
@@ -373,13 +415,20 @@
         sent_p(3, p, ret2.at[p, 1, top])
         sent_p(8, p, ret2.at[p, 0, top])
         sent_p(9, p, ret2.at[p, 1, bottom])
-        sent_p(4, p, coef.at[p, 1])
-        sent_p(5, p, coef.at[p, 2])
-        sent_p(6, p, coef.at[p, 3, top])
-        sent_p(7, p, coef.at[p, 3, bottom])
         return carry
 
     lax.fori_loop(0, 3, drain_p, 0)
+    sent_p(4, 0, coef.at[0, 1])
+    sent_p(5, 0, coef.at[0, 2])
+    sent_p(6, 0, coef.at[0, 3, top])
+    sent_p(7, 0, coef.at[0, 3, bottom])
+
+    def drain_s(i, carry):
+        for kind in range(3):
+            done_s(s_send, kind, i, coef.at[1, kind, pl.ds(0, strip)])
+        return carry
+
+    lax.fori_loop(0, 2 * per, drain_s, 0)
 
 
 def local(spectra, tables, apodization, inv_mask, weights):
@@ -420,6 +469,8 @@
             pltpu.SemaphoreType.DMA((21, chunks)),
             pltpu.SemaphoreType.DMA((10, 3)),
             pltpu.SemaphoreType.DMA((10, 3)),
+            pltpu.SemaphoreType.DMA((3, 2 * chunks // 3)),
+            pltpu.SemaphoreType.DMA((3, 2 * chunks // 3)),
         ],
         compiler_params=pltpu.CompilerParams(
             collective_id=0, has_side_effects=True, vmem_limit_bytes=60 * 1024 * 1024),

time: 130 us -> 130 us (level)
  no operation moved by 1% of the time
where the time goes in v4:
time: 130 us
  Pallas kernels  128 us (98%)
  local copies, waits for them, and re-layouts  1.92 us (1%)
    pallas_call x1, Pallas kernels, local(): pl.pallas_call(kernel, out_shape=jax.ShapeDtypeStruct(spectra.shape, F32)...  128 us

profile of v4, /device:TPU:0, one launch (start us, length us, event | category | flops | bytes accessed | tf_op | source)
XLA Modules:
  0.0 130.2 jit_solution(11938093970281286699)
XLA Ops:
  0.0 128.2 %shard_map.55 = f32[3,192,224]{2,1,0:T(8,128)} custom-call(f32[3,192,224]{2,1,0:T(8,128)} %spec.1, f32[3,192,6144]{2,1,0:T(8,128)} %tables.1, f32[1,6144]{1,0:T(1,128)} %bitcast.3, f32[1,6144]{1,0:T(1,128)} %bitcast.4, f32[1,6144]{1,0:T(1,128)} %bitcast.5), custom_call_target="tpu_custom_call" | custom-call | tf_op jit(solution)/shard_map/pallas_call | solution.py:446
  128.2 1.9 %copy.7 = f32[3,192,224]{2,1,0:T(8,128)} copy(f32[3,192,224]{2,1,0:T(8,128)} %shard_map.55) | data formatting | bytes 1032192

commit v5 on v4

--- a/solution.py
+++ b/solution.py
@@ -11,10 +11,10 @@
     "share", "back", "cross", "spread", "corr", "ret_fold", "fold", "total", "relay",
     "ret_sum", "pass_on", "ret", "send", "scale",
 )
-LEAD, FIRST, DIRECT, STRIP_LAG = 2, 1, 3, 2
+LEAD, FIRST, DIRECT, STRIP_LAG = 3, 1, 3, 2
 DELAY = dict(
     relay=0, share=2, pass_on=3, corr=4, fold=5, total=6, cross=8, scale=9, spread=11,
-    back=13, ret=13, ret_fold=15, ret_sum=17, send=-2,
+    back=13, ret=13, ret_fold=15, ret_sum=17, send=-3,
 )
 F32, BF16 = jnp.float32, jnp.bfloat16
 

time: 130 us -> 132 us (1.015)
  Pallas kernels: 128 us -> 130 us
    pallas_call x1, Pallas kernels: 128 us -> 130 us  [local(): pl.pallas_call(kernel, out_shape=jax.ShapeDtypeStruct(spectra.shape, F32)...]
where the time goes in v5:
time: 132 us
  Pallas kernels  130 us (98%)
  local copies, waits for them, and re-layouts  1.92 us (1%)
    pallas_call x1, Pallas kernels, local(): pl.pallas_call(kernel, out_shape=jax.ShapeDtypeStruct(spectra.shape, F32)...  130 us

profile of v5, /device:TPU:0, one launch (start us, length us, event | category | flops | bytes accessed | tf_op | source)
XLA Modules:
  0.0 131.6 jit_solution(7186543338970937369)
XLA Ops:
  0.0 129.6 %shard_map.55 = f32[3,192,224]{2,1,0:T(8,128)} custom-call(f32[3,192,224]{2,1,0:T(8,128)} %spec.1, f32[3,192,6144]{2,1,0:T(8,128)} %tables.1, f32[1,6144]{1,0:T(1,128)} %bitcast.3, f32[1,6144]{1,0:T(1,128)} %bitcast.4, f32[1,6144]{1,0:T(1,128)} %bitcast.5), custom_call_target="tpu_custom_call" | custom-call | tf_op jit(solution)/shard_map/pallas_call | solution.py:446
  129.6 1.9 %copy.7 = f32[3,192,224]{2,1,0:T(8,128)} copy(f32[3,192,224]{2,1,0:T(8,128)} %shard_map.55) | data formatting | bytes 1032192
